TPU v7x, 256 devices: a whole 4x4x8 slice. The times are simulated.
256 devices in a mesh: leaf: 64 (over z, y, core), hand: 4 (over x).
Axes of the slice: x: 4, y: 4, z: 8, core: 2. Of those that a mesh axis runs over, the one named last changes fastest.
Arguments:
- opp_range: float32 [1024], P('hand'), may hold values from 0.1 to 1
- br_range: float32 [1024], P('hand'), may hold values from 0.001 to 1
- up_weight: bfloat16 [4, 2048, 1024], P(None, 'leaf', 'hand'), may hold values from 0.29882812 to 1
- up_parent: int32 [3, 2048], replicated, may hold values from 0 to 2047
- board_cards: int32 [6144, 5], P('leaf'), may hold values from 0 to 51, as said below
- hand_rank: int32 [6144, 1024], P('leaf'), may hold values from 0 to 7461
- root_parent: int32 [6144], P('leaf'), may hold values from 0 to 2047
- br_actions: int32 [6144], P('leaf'), may hold values from 1 to 8
- opp_actions: int32 [6144, 8], P('leaf'), may hold values from 1 to 8
- leaf_kind: int32 [6144, 8, 8], P('leaf'), may hold values from 0 to 1
- leaf_stake: int32 [6144, 8, 8], P('leaf'), may hold values from 1 to 400
- opp_weight: bfloat16 [6144, 8, 8, 1024], P('leaf', None, None, 'hand'), may hold values from 0.049804688 to 1
Outputs:
- level_values: float32 [4, 2048, 1024], P(None, 'leaf', 'hand')
- root_value: float32 [1024], P('hand')
- best_value: float32 [], replicated
Inputs may be any that keep to these rules, and one draw needn't show every extreme that they name: `board_cards`: five different cards for each subtree.
All inputs are finite; a program needn't handle non-finite values.
Results may differ from a plain program's by a relative error of at most 0.0003.
Values may be sent and summed in bfloat16 or wider, within the bound.
A program may use at most 128 MiB of HBM per device.

v0:
```python
import jax
import jax.numpy as jnp
import numpy as np
from jax import lax
from jax.sharding import Mesh
from jax.sharding import PartitionSpec as P

LEAF = ("leaf_0", "leaf_1", "leaf_2")
PAYOFF_UNIT = 1.0 / 4096.0


def laid_out(parts, dim):
    parts = jnp.moveaxis(parts, 0, dim)
    lengths = parts.shape
    return parts.reshape(*lengths[:dim], lengths[dim] * lengths[dim + 1], *lengths[dim + 2 :])


def all_blocks(x, axes, turns):
    parts = x[None]
    for k in turns:
        parts = lax.all_gather(parts, axes[k], axis=0, tiled=True)
    carried = [lax.axis_size(axes[k]) for k in reversed(turns)]
    parts = parts.reshape(*carried, *x.shape)
    turned = sorted(range(len(turns)), key=lambda place: turns[len(turns) - 1 - place])
    return parts.transpose(*turned, *range(len(turns), parts.ndim)).reshape(-1, *x.shape)


def whole_of(x, axes, turns, dim):
    return laid_out(all_blocks(x, axes, turns), dim)


def split_up(x, dim, devices):
    before, after = (x.shape[:dim], x.shape[dim + 1 :])
    return jnp.moveaxis(x.reshape(*before, devices, -1, *after), dim, 0)


def summed_on_arrival(x, axis, dim):
    parts = split_up(x, dim, lax.axis_size(axis))
    arrived = lax.all_to_all(parts, axis, split_axis=0, concat_axis=0, tiled=True)
    return arrived.sum(axis=0)


def copy_for_each(x, axis):
    devices = lax.axis_size(axis)
    return lax.all_to_all(jnp.broadcast_to(x[None], (devices, *x.shape)), axis, 0, 0, tiled=True)


def gather_directly(x, axis, dim):
    return laid_out(copy_for_each(x, axis), dim)


def of_everyone(x, axis):
    everything = copy_for_each(x, axis)
    return jnp.sum(everything, axis=0)


def hand_cards(number):
    low_list = []
    high_list = []
    for low_card in range(52):
        for high_card in range(low_card + 1, 52):
            low_list.append(low_card)
            high_list.append(high_card)
    chosen = np.arange(number) * 1326 // number
    return (np.array(low_list, np.int32)[chosen], np.array(high_list, np.int32)[chosen])


def no_shared(low_rows, high_rows, low_cols, high_cols):
    apart_mask = (low_rows[:, None] != low_cols[None, :]) & (
        low_rows[:, None] != high_cols[None, :]
    )
    apart_mask = (
        apart_mask
        & (high_rows[:, None] != low_cols[None, :])
        & (high_rows[:, None] != high_cols[None, :])
    )
    return apart_mask.astype(jnp.float32)


def board_compat(board_cards, low_cols, high_cols):
    hits = (board_cards[:, :, None] == low_cols[None, None, :]) | (
        board_cards[:, :, None] == high_cols[None, None, :]
    )
    return 1.0 - jnp.any(hits, axis=1).astype(jnp.float32)


def local(
    opp_range,
    br_range,
    up_weight,
    up_parent,
    board_cards,
    hand_rank,
    root_parent,
    br_actions,
    opp_actions,
    leaf_kind,
    leaf_stake,
    opp_weight,
):
    levels_count = up_weight.shape[0]
    nodes_dev = up_weight.shape[1]
    hands_dev = opp_range.shape[0]
    boards_dev = board_cards.shape[0]
    actions_max = opp_actions.shape[1]
    hands_all = hand_rank.shape[1]
    node_total = nodes_dev * lax.axis_size(LEAF)
    node_start = lax.axis_index(LEAF) * nodes_dev
    hand_start = lax.axis_index("hand") * hands_dev
    low_np, high_np = hand_cards(hands_all)
    low_all = jnp.asarray(low_np)
    high_all = jnp.asarray(high_np)
    low_mine = lax.dynamic_slice_in_dim(low_all, hand_start, hands_dev)
    high_mine = lax.dynamic_slice_in_dim(high_all, hand_start, hands_dev)
    compat = board_compat(board_cards, low_mine, high_mine)
    weights = whole_of(up_weight, LEAF, (1, 0, 2), 1)
    gathered = opp_range[None, :] * weights[0].astype(jnp.float32)
    for level_id in range(1, levels_count):
        gathered = jnp.take(gathered, up_parent[level_id - 1], axis=0) * weights[level_id].astype(
            jnp.float32
        )
    root_reach = jnp.take(gathered, root_parent, axis=0) * compat
    legal_mask = (jnp.arange(actions_max)[None, None, :] < opp_actions[:, :, None]).astype(
        jnp.float32
    )
    weighted = opp_weight.astype(jnp.float32) * legal_mask[..., None]
    probability = weighted / jnp.sum(weighted, axis=2, keepdims=True)
    leaf_reach = (root_reach[:, None, None, :] * probability).astype(jnp.bfloat16)
    leaf_reach = leaf_reach.reshape(boards_dev, actions_max * actions_max, hands_dev)
    kind_flat = leaf_kind.reshape(boards_dev, -1)
    stake_flat = leaf_stake.reshape(boards_dev, -1).astype(jnp.float32) * PAYOFF_UNIT
    rank_mine = lax.dynamic_slice_in_dim(hand_rank, hand_start, hands_dev, 1)
    zero_block = jnp.zeros(leaf_reach.shape, jnp.float32)
    block_rows = lax.all_gather(leaf_reach, "hand", axis=2, tiled=True)
    count_rows = block_rows.shape[2]
    low_rows = lax.slice_in_dim(low_all, 0, count_rows, axis=0)
    high_rows = lax.slice_in_dim(high_all, 0, count_rows, axis=0)
    apart_mask = no_shared(low_rows, high_rows, low_mine, high_mine).astype(jnp.bfloat16)
    order_sign = (
        jnp.sign(rank_mine[:, None, :] - hand_rank[:, :, None]).astype(jnp.bfloat16)
        * apart_mask[None]
    )
    showdown = zero_block + jnp.einsum(
        "blo,boh->blh", block_rows, order_sign, preferred_element_type=jnp.float32
    )
    folded = zero_block + jnp.einsum(
        "blo,oh->blh", block_rows, apart_mask, preferred_element_type=jnp.float32
    )
    showdown, folded = (showdown, folded)
    payoff = (
        jnp.where(kind_flat[:, :, None] == 1, showdown, folded)
        * stake_flat[:, :, None]
        * compat[:, None, :]
    )
    per_node = jnp.sum(payoff.reshape(boards_dev, actions_max, actions_max, hands_dev), axis=2)
    allowed = jnp.arange(actions_max)[None, :, None] < br_actions[:, None, None]
    sub_value = jnp.max(jnp.where(allowed, per_node, -1e30), axis=1)
    contrib = jax.ops.segment_sum(sub_value, root_parent, num_segments=node_total)
    last_mine = summed_on_arrival(contrib, LEAF, 0)
    whole_level = gather_directly(last_mine, LEAF, 0)
    level_list = [last_mine]
    for level_id in range(levels_count - 1, 0, -1):
        whole_level = jax.ops.segment_sum(
            whole_level, up_parent[level_id - 1], num_segments=node_total
        )
        level_list.insert(0, lax.dynamic_slice_in_dim(whole_level, node_start, nodes_dev))
    level_values = jnp.stack(level_list)
    local_total = jnp.sum(level_values[0], axis=0)
    root_value = of_everyone(local_total, LEAF) / node_total
    weighted_sum, range_total = lax.psum(
        (jnp.sum(br_range * root_value), jnp.sum(br_range)), "hand"
    )
    best_value = weighted_sum / range_total
    return (level_values, root_value, best_value)


def solution(mesh):
    split = Mesh(
        mesh.devices.reshape(8, 4, 2, mesh.shape["hand"]), ("leaf_0", "leaf_1", "leaf_2", "hand")
    )
    in_specs = (
        P("hand"),
        P("hand"),
        P(None, LEAF, "hand"),
        P(),
        P(LEAF, None),
        P(LEAF, None),
        P(LEAF),
        P(LEAF),
        P(LEAF, None),
        P(LEAF, None, None),
        P(LEAF, None, None),
        P(LEAF, None, None, "hand"),
    )
    out_specs = (P(None, LEAF, "hand"), P("hand"), P())
    return jax.shard_map(local, mesh=split, in_specs=in_specs, out_specs=out_specs, check_vma=False)
```

profile of v0, /device:TPU:1, one launch (start us, length us, event | category | flops | bytes accessed | tf_op | source)
XLA Modules:
  0.0 494.6 jit_solution(5926093371873539124)
XLA Ops:
  7.3 12.7 %all-gather = bf16[16,32,256]{2,1,0:T(8,128)(2,1)} all-gather(bf16[4,32,256]{2,1,0:T(8,128)(2,1)} %param.18), channel_id=2, replica_groups=mesh['leaf_0'=8,'leaf_1'=4,'leaf_2'=2,'hand'=4] {'leaf_1'}, dimensions={0}, use_global_device_ids=true | all-gather | bytes 327680 | tf_op jit(solution)/shard_map/all_gather | solution.py:21
  20.0 40.9 %all-gather.5.cloned.1.call-done = bf16[32,4,32,256]{3,2,1,0:T(8,128)(2,1)} async-done(((bf16[4,4,32,256]{3,2,1,0:T(8,128)(2,1)}), bf16[32,4,32,256]{3,2,1,0:T(8,128)(2,1)}) %all-gather.5.cloned.1.call-update) | async-done | bytes 2097168 | tf_op jit(solution)/shard_map/all_gather | solution.py:21
  61.0 0.8 dynamic_slice.18
  61.8 0.8 dynamic_slice.19
  62.6 0.6 pad_clamp_fusion
  63.2 0.8 or_reduce_fusion
  64.0 0.5 compare_and_fusion.3
  64.6 0.6 compare_and_fusion.2
  65.2 0.6 compare_and_fusion.1
  65.8 0.6 compare_and_fusion
  66.4 0.6 fusion.23
  67.0 0.6 fusion.24
  67.5 0.6 fusion.25
  68.3 16.9 %all-gather.7.cloned.1.call-done = bf16[64,4,32,256]{3,2,1,0:T(8,128)(2,1)} async-done(((bf16[32,4,32,256]{3,2,1,0:T(8,128)(2,1)}), bf16[64,4,32,256]{3,2,1,0:T(8,128)(2,1)}) %all-gather.7.cloned.1.call-update) | async-done | bytes 4194320 | tf_op jit(solution)/shard_map/all_gather | solution.py:21
  85.2 2.6 copy.32
  87.9 1.7 fusion.27
  89.8 9.3 %gather_fusion.1 = f32[2048,256]{1,0:T(8,128)} fusion(f32[2048,256]{1,0:T(8,128)S(1)} %convert_multiply_fusion.5, s32[2048]{0:T(1024)} %fusion.23), kind=kCustom, calls=%fused_computation.clone | custom fusion | bytes 4202496 | tf_op jit(solution)/shard_map/jit(_take)/gather | solution.py:119
  99.1 2.1 convert_multiply_fusion.4
  101.3 9.3 %gather_fusion.2 = f32[2048,256]{1,0:T(8,128)} fusion(f32[2048,256]{1,0:T(8,128)S(1)} %convert_multiply_fusion.4, s32[2048]{0:T(1024)} %fusion.24), kind=kCustom, calls=%fused_computation.1.clone | custom fusion | bytes 4202496 | tf_op jit(solution)/shard_map/jit(_take)/gather | solution.py:119
  110.5 2.1 convert_multiply_fusion.3
  112.7 9.3 %gather_fusion.3 = f32[2048,256]{1,0:T(8,128)} fusion(f32[2048,256]{1,0:T(8,128)S(1)} %convert_multiply_fusion.3, s32[2048]{0:T(1024)} %fusion.25), kind=kCustom, calls=%fused_computation.2.clone | custom fusion | bytes 4202496 | tf_op jit(solution)/shard_map/jit(_take)/gather | solution.py:119
  122.0 1.8 convert_multiply_fusion.2
  123.8 0.8 gather_fusion
  124.6 0.8 convert_subtract_fusion
  125.4 6.9 %fusion.9 = bf16[96,64,256]{2,1,0:T(8,128)(2,1)} fusion(f32[96,8,8]{2,1,0:T(8,128)S(1)} %fusion.22, bf16[96,8,8,256]{3,2,1,0:T(8,128)(2,1)} %param.27, f32[96,256]{1,0:T(8,128)S(1)} %get-tuple-element.19), kind=kOutput, calls=%fused_computation.20 | output fusion | flops 11206663 | bytes 6414336 | tf_op jit(solution)/shard_map/div | solution.py:127
  132.4 0.7 copy-done.3
  133.5 0.7 convert_convert_fusion
  134.2 122.0 %all-gather.9.cloned.1.call-done = bf16[96,64,1024]{2,1,0:T(8,128)(2,1)} async-done(((bf16[96,64,256]{2,1,0:T(8,128)(2,1)}), bf16[96,64,1024]{2,1,0:T(8,128)(2,1)}) %all-gather.9.cloned.1.call-update) | async-done | bytes 12582928 | tf_op jit(solution)/shard_map/all_gather | solution.py:134
  256.3 8.5 %fusion.20 = f32[96,64,256]{2,1,0:T(8,128)S(1)} fusion(bf16[96,64,1024]{2,1,0:T(8,128)(2,1)} %all-gather.9.cloned.1.call-done, s32[256]{0:T(256)S(1)} %copy-done.9, s32[256]{0:T(256)S(1)} %copy-done.7, s32[1024]{0:T(1024)S(1)} %copy-done.11, s32[1024]{0:T(1024)S(1)} %copy-done.10), kind=kOutput, calls=%fused_computation.35 | convolution fusion | flops 3223584768 | bytes 18884608 | tf_op jit(solution)/shard_map/blo,oh->blh/dot_general | solution.py:146
  264.8 28.5 %bitcast_reduce_fusion = f32[96,8,256]{2,1,0:T(8,128)S(1)} fusion(f32[96,64,256]{2,1,0:T(8,128)S(1)} %fusion.20, f32[96,256]{1,0:T(8,128)S(1)} %get-tuple-element.18, f32[96,64]{1,0:T(8,128)S(1)} %copy.34, pred[96,64]{1,0:T(8,128)(4,1)S(1)} %copy.31, bf16[96,64,1024]{2,1,0:T(8,128)(2,1)S(1)} %copy-done.17, s32[96,1024]{1,0:T(8,128)S(1)} %copy-done.4, ...), kind=kOutput, calls=%fused_computation.15 | convolution fusion | flops 3327983616 | bytes 20805632 | tf_op jit(solution)/shard_map/blo,boh->blh/dot_general | solution.py:143
  293.6 1.7 scatter_custom_fusion
  295.3 62.1 %all_to_all.16 = f32[64,32,256]{2,1,0:T(8,128)} all-to-all(f32[64,32,256]{2,1,0:T(8,128)S(1)} %bitcast.47), channel_id=1, replica_groups=mesh['leaf_0'=8,'leaf_1'=4,'leaf_2'=2,'hand'=4] {'leaf_0','leaf_1','leaf..., dimensions={0} | all-to-all | bytes 4194304 | tf_op jit(solution)/shard_map/all_to_all | solution.py:39
  357.4 1.7 reduce_sum.65
  359.1 1.6 broadcast_in_dim.59
  360.7 7.0 %all-to-all-start.1 = ((f32[64,32,256]{2,1,0:T(8,128)}), f32[64,32,256]{2,1,0:T(8,128)S(1)}, u32[]{:S(2)}, u32[]{:S(2)}) async-start(f32[64,32,256]{2,1,0:T(8,128)} %broadcast_in_dim.59), calls=%async_computation.1 | async-start | bytes 4194304 | tf_op jit(solution)/shard_map/all_to_all | solution.py:45
  367.7 49.7 %all-to-all-done.1 = f32[64,32,256]{2,1,0:T(8,128)S(1)} async-done(((f32[64,32,256]{2,1,0:T(8,128)}), f32[64,32,256]{2,1,0:T(8,128)S(1)}, u32[]{:S(2)}, u32[]{:S(2)}) %all-to-all-start.1) | async-done | bytes 2097184 | tf_op jit(solution)/shard_map/all_to_all | solution.py:45
  417.4 1.3 copy-done
  418.7 12.5 %scatter_custom_fusion.1 = f32[2048,256]{1,0:T(8,128)S(1)} fusion(s32[2048]{0:T(1024)} %bitcast.60, f32[2048,256]{1,0:T(8,128)} %bitcast.49, f32[]{:T(128)} %constant.20.clone.1), kind=kCustom, calls=%fused_computation.30 | custom fusion | flops 524288 | bytes 2097664 | tf_op jit(solution)/shard_map/scatter-add | solution.py:163
  431.2 13.0 %scatter_custom_fusion.2 = f32[2048,256]{1,0:T(8,128)} fusion(s32[2048]{0:T(1024)S(1)} %bitcast.57, f32[2048,256]{1,0:T(8,128)S(1)} %scatter_custom_fusion.1, f32[]{:T(128)} %constant.20.clone.1), kind=kCustom, calls=%fused_computation.28 | custom fusion | flops 524288 | bytes 2097156 | tf_op jit(solution)/shard_map/scatter-add | solution.py:163
  444.2 13.3 %scatter_custom_fusion.3 = f32[2048,256]{1,0:T(8,128)} fusion(s32[2048]{0:T(1024)S(1)} %bitcast.54, f32[2048,256]{1,0:T(8,128)} %scatter_custom_fusion.2, f32[]{:T(128)} %constant.20.clone.1), kind=kCustom, calls=%fused_computation.26 | custom fusion | flops 524288 | bytes 2097664 | tf_op jit(solution)/shard_map/scatter-add | solution.py:163
  457.5 0.8 dynamic-slice_reduce_fusion
  458.3 0.7 broadcast_in_dim.96
  459.0 7.0 %all-to-all-start.2 = ((f32[64,1,256]{2,1,0:T(1,128)}), f32[64,1,256]{2,1,0:T(1,128)S(1)}, u32[]{:S(2)}, u32[]{:S(2)}) async-start(f32[64,1,256]{2,1,0:T(1,128)} %broadcast_in_dim.96), calls=%async_computation.2 | async-start | bytes 131072 | tf_op jit(solution)/shard_map/all_to_all | solution.py:45
  465.9 0.8 dynamic-slice_bitcast_fusion
  466.7 0.7 pad_maximum_fusion
  467.4 8.6 %all-to-all-done.2 = f32[64,1,256]{2,1,0:T(1,128)S(1)} async-done(((f32[64,1,256]{2,1,0:T(1,128)}), f32[64,1,256]{2,1,0:T(1,128)S(1)}, u32[]{:S(2)}, u32[]{:S(2)}) %all-to-all-start.2) | async-done | bytes 65568 | tf_op jit(solution)/shard_map/all_to_all | solution.py:45
  476.1 1.2 fusion.26
  477.3 8.4 %all-reduce = (f32[]{:T(128)}, f32[]{:T(128)}) all-reduce(f32[]{:T(128)} %get-tuple-element.5, f32[]{:T(128)} %get-tuple-element.4), channel_id=1, replica_groups=mesh['leaf_0'=8,'leaf_1'=4,'leaf_2'=2,'hand'=4] {'hand'}, use_global_device_ids=true, to_apply=%region_12.14 | all-reduce | flops 2 | bytes 16 | tf_op jit(solution)/shard_map/psum | solution.py:170
  (55 shorter events, 1.5 us)
Async XLA Ops:
  7.2 55.4 %copy-start.13 = (s32[96,8]{0,1:T(8,128)S(1)}, s32[96,8]{0,1:T(8,128)}, u32[]{:S(2)}) copy-start(s32[96,8]{0,1:T(8,128)} %param.24) | copy-start | bytes 9220
  7.2 55.4 %copy-start.18 = (s32[96]{0:T(128)S(1)}, s32[96]{0:T(128)}, u32[]{:S(2)}) copy-start(s32[96]{0:T(128)} %param.22) | copy-start | bytes 1156
  7.2 56.0 %copy-start.12 = (s32[96,5]{0,1:T(8,128)S(1)}, s32[96,5]{0,1:T(8,128)}, u32[]{:S(2)}) copy-start(s32[96,5]{0,1:T(8,128)} %param.20) | copy-start | bytes 5764
  7.2 57.4 %copy-start.5 = (s32[3,2048]{1,0:T(4,128)S(1)}, s32[3,2048]{1,0:T(4,128)}, u32[]{:S(2)}) copy-start(s32[3,2048]{1,0:T(4,128)} %param.19) | copy-start | bytes 73732
  7.2 53.7 %all-gather.5.cloned.1.call-start = ((), (), s32[]{:S(2)}) async-start(), calls=%async_computation.3 | async-start | bytes 2359296 | tf_op jit(solution)/shard_map/all_gather | solution.py:21
  19.9 65.3 %all-gather.7.cloned.1.call-start = ((), (), s32[]{:S(2)}) async-start(), calls=%async_computation.4 | async-start | bytes 6291456 | tf_op jit(solution)/shard_map/all_gather | solution.py:21
  60.9 195.3 %all-gather.9.cloned.1.call-start = ((), (), s32[]{:S(2)}) async-start(), calls=%async_computation.5 | async-start | bytes 15728640 | tf_op jit(solution)/shard_map/all_gather | solution.py:134
  61.8 2.3 copy-start.6
  62.5 1.5 copy-start.8
  64.6 23.3 %copy-start.1 = (s32[1,2048]{1,0:T(1,128)}, s32[1,2048]{1,0:T(1,128)S(1)}, u32[]{:S(2)}) copy-start(s32[1,2048]{1,0:T(1,128)S(1)} %get-tuple-element.15) | copy-start | bytes 24580
  87.9 1.8 copy-start.14
  132.3 0.8 copy-start.3
  132.3 0.9 copy-start.2
  132.3 1.0 copy-start.4
  132.3 1.0 copy-start.16
  132.3 1.1 copy-start.7
  132.4 1.1 copy-start.9
  132.4 1.1 copy-start.10
  132.4 1.1 copy-start.11
  256.3 8.5 %copy-start.17 = (bf16[96,64,1024]{2,1,0:T(8,128)(2,1)S(1)}, bf16[96,64,1024]{2,1,0:T(8,128)(2,1)}, u32[]{:S(2)}) copy-start(bf16[96,64,1024]{2,1,0:T(8,128)(2,1)} %all-gather.9.cloned.1.call-done) | copy-start | bytes 37748740
  360.7 56.7 %all-to-all-start.1 = ((f32[64,32,256]{2,1,0:T(8,128)}), f32[64,32,256]{2,1,0:T(8,128)S(1)}, u32[]{:S(2)}, u32[]{:S(2)}) async-start(f32[64,32,256]{2,1,0:T(8,128)} %broadcast_in_dim.59), calls=%async_computation.1 | async-start | bytes 4194304 | tf_op jit(solution)/shard_map/all_to_all | solution.py:45
  417.4 1.4 copy-start
  431.2 44.9 %copy-start.15 = (f32[256]{0:T(256)S(1)}, f32[256]{0:T(256)}, u32[]{:S(2)}) copy-start(f32[256]{0:T(256)} %param.17) | copy-start | bytes 3076
  459.0 17.0 %all-to-all-start.2 = ((f32[64,1,256]{2,1,0:T(1,128)}), f32[64,1,256]{2,1,0:T(1,128)S(1)}, u32[]{:S(2)}, u32[]{:S(2)}) async-start(f32[64,1,256]{2,1,0:T(1,128)} %broadcast_in_dim.96), calls=%async_computation.2 | async-start | bytes 131072 | tf_op jit(solution)/shard_map/all_to_all | solution.py:45
Sparse Core Ops, SparseCore 0:
  20.1 40.8 all-gather.4
  62.7 22.4 all-gather.6
  132.5 123.6 all-gather.8
where the time goes:
time: 496 us; the launch traced here: 495 us
  waiting for transfers between devices  238 us (48%)
  blocking collectives  83.1 us (17%)
  other arithmetic  65.8 us (13%)
  local copies, waits for them, and re-layouts  40.1 us (8%)
  matrix products  37 us (7%)
  between operations  16.5 us (3%)
  starting transfers between devices  14 us (3%)
    all_gather x1, waiting for transfers between devices, local(): block_rows = lax.all_gather(leaf_reach, 'hand', axis=2, tiled=True)  122 us
    all_to_all x1, blocking collectives, summed_on_arrival(): lax.all_to_all(parts, axis, split_axis=0, concat_axis=0, tiled=True)  62.1 us
    all_to_all x2, waiting for transfers between devices, copy_for_each(): lax.all_to_all(jnp.broadcast_to(x[None], (devices, *x.shape)), axis, 0, 0...  58.3 us
    all_gather x2, waiting for transfers between devices, all_blocks(): parts = lax.all_gather(parts, axes[k], axis=0, tiled=True)  57.8 us
    scatter-add x3, other arithmetic, local(): jax.ops.segment_sum(whole_level, up_parent[level_id - 1], num_segments=no...  38.8 us
    dot_general x1, matrix products, local(): jnp.einsum('blo,boh->blh', block_rows, order_sign, preferred_element_type...  28.5 us
    gather x3, local copies, waits for them, and re-layouts, local(): jnp.take(gathered, up_parent[level_id - 1], axis=0)  27.9 us
    all_to_all x2, starting transfers between devices, copy_for_each(): lax.all_to_all(jnp.broadcast_to(x[None], (devices, *x.shape)), axis, 0, 0...  13.9 us
  transfers between devices with their start and end apart: 5, of which 5 were waited for; matrix products, arithmetic and copies ran while one was open for 2% of the time, Pallas kernels for 0%

commit v1 on v0

--- a/solution.py
+++ b/solution.py
@@ -7,6 +7,12 @@
 
 LEAF = ("leaf_0", "leaf_1", "leaf_2")
 PAYOFF_UNIT = 1.0 / 4096.0
+
+
+def gather_by_exchange(x, axis, dim):
+    count = lax.axis_size(axis)
+    repeats = [count if d == dim else 1 for d in range(x.ndim)]
+    return lax.all_to_all(jnp.tile(x, repeats), axis, split_axis=dim, concat_axis=dim, tiled=True)
 
 
 def laid_out(parts, dim):
@@ -131,7 +137,7 @@
     stake_flat = leaf_stake.reshape(boards_dev, -1).astype(jnp.float32) * PAYOFF_UNIT
     rank_mine = lax.dynamic_slice_in_dim(hand_rank, hand_start, hands_dev, 1)
     zero_block = jnp.zeros(leaf_reach.shape, jnp.float32)
-    block_rows = lax.all_gather(leaf_reach, "hand", axis=2, tiled=True)
+    block_rows = gather_by_exchange(leaf_reach, "hand", 2)
     count_rows = block_rows.shape[2]
     low_rows = lax.slice_in_dim(low_all, 0, count_rows, axis=0)
     high_rows = lax.slice_in_dim(high_all, 0, count_rows, axis=0)

time: 496 us -> 599 us (1.21)
  waiting for transfers between devices: 238 us -> 298 us
  local copies, waits for them, and re-layouts: 40.1 us -> 77.5 us
  starting transfers between devices: 14 us -> 21.3 us
    all_to_all x0 -> x1, waiting for transfers between devices: none -> 182 us  [gather_by_exchange(): lax.all_to_all(jnp.tile(x, repeats), axis, split_axis=dim, concat_axis=di...]
    all_gather x1 -> x0, waiting for transfers between devices: 122 us -> none  [local(): block_rows = lax.all_gather(leaf_reach, 'hand', axis=2, tiled=True)]
    all_to_all x0 -> x1, local copies, waits for them, and re-layouts: none -> 25 us  [gather_by_exchange(): lax.all_to_all(jnp.tile(x, repeats), axis, split_axis=dim, concat_axis=di...]
    another operation x0 -> x2, local copies, waits for them, and re-layouts: none -> 13.1 us  [gather_by_exchange(): jnp.tile(x, repeats)]
    all_to_all x0 -> x1, starting transfers between devices: none -> 7.28 us  [gather_by_exchange(): lax.all_to_all(jnp.tile(x, repeats), axis, split_axis=dim, concat_axis=di...]
where the time goes in v1:
time: 599 us; the launch traced here: 597 us
  waiting for transfers between devices  298 us (50%)
  blocking collectives  80.6 us (13%)
  local copies, waits for them, and re-layouts  77.5 us (13%)
  other arithmetic  65.1 us (11%)
  matrix products  37 us (6%)
  starting transfers between devices  21.3 us (4%)
  between operations  16.8 us (3%)
    all_to_all x1, waiting for transfers between devices, gather_by_exchange(): lax.all_to_all(jnp.tile(x, repeats), axis, split_axis=dim, concat_axis=di...  182 us
    all_to_all x1, blocking collectives, summed_on_arrival(): lax.all_to_all(parts, axis, split_axis=0, concat_axis=0, tiled=True)  60.4 us
    all_to_all x2, waiting for transfers between devices, copy_for_each(): lax.all_to_all(jnp.broadcast_to(x[None], (devices, *x.shape)), axis, 0, 0...  58.3 us
    all_gather x2, waiting for transfers between devices, all_blocks(): parts = lax.all_gather(parts, axes[k], axis=0, tiled=True)  57.9 us
    scatter-add x3, other arithmetic, local(): jax.ops.segment_sum(whole_level, up_parent[level_id - 1], num_segments=no...  38.8 us
    dot_general x1, matrix products, local(): jnp.einsum('blo,boh->blh', block_rows, order_sign, preferred_element_type...  28.5 us
    gather x3, local copies, waits for them, and re-layouts, local(): jnp.take(gathered, up_parent[level_id - 1], axis=0)  27.9 us
    all_to_all x1, local copies, waits for them, and re-layouts, gather_by_exchange(): lax.all_to_all(jnp.tile(x, repeats), axis, split_axis=dim, concat_axis=di...  25 us
  transfers between devices with their start and end apart: 5, of which 5 were waited for; matrix products, arithmetic and copies ran while one was open for 2% of the time, Pallas kernels for 0%

profile of v1, /device:TPU:1, one launch (start us, length us, event | category | flops | bytes accessed | tf_op | source)
XLA Modules:
  0.0 596.8 jit_solution(458986123444705487)
XLA Ops:
  7.3 12.7 %all-gather = bf16[16,32,256]{2,1,0:T(8,128)(2,1)} all-gather(bf16[4,32,256]{2,1,0:T(8,128)(2,1)} %param.18), channel_id=2, replica_groups=mesh['leaf_0'=8,'leaf_1'=4,'leaf_2'=2,'hand'=4] {'leaf_1'}, dimensions={0}, use_global_device_ids=true | all-gather | bytes 327680 | tf_op jit(solution)/shard_map/all_gather | solution.py:27
  20.0 40.9 %all-gather.4.cloned.1.call-done = bf16[32,4,32,256]{3,2,1,0:T(8,128)(2,1)} async-done(((bf16[4,4,32,256]{3,2,1,0:T(8,128)(2,1)}), bf16[32,4,32,256]{3,2,1,0:T(8,128)(2,1)}) %all-gather.4.cloned.1.call-update) | async-done | bytes 2097168 | tf_op jit(solution)/shard_map/all_gather | solution.py:27
  60.9 0.8 dynamic_slice.18
  61.7 0.8 dynamic_slice.19
  62.6 0.6 pad_clamp_fusion
  63.2 0.8 or_reduce_fusion
  65.7 0.6 compare_and_fusion
  66.2 0.6 fusion.23
  66.9 0.6 fusion.24
  67.4 0.6 fusion.25
  68.2 17.0 %all-gather.6.cloned.1.call-done = bf16[64,4,32,256]{3,2,1,0:T(8,128)(2,1)} async-done(((bf16[32,4,32,256]{3,2,1,0:T(8,128)(2,1)}), bf16[64,4,32,256]{3,2,1,0:T(8,128)(2,1)}) %all-gather.6.cloned.1.call-update) | async-done | bytes 4194320 | tf_op jit(solution)/shard_map/all_gather | solution.py:27
  85.2 2.6 copy.46
  87.9 1.7 fusion.27
  89.8 9.3 %gather_fusion.1 = f32[2048,256]{1,0:T(8,128)} fusion(f32[2048,256]{1,0:T(8,128)S(1)} %convert_multiply_fusion.5, s32[2048]{0:T(1024)} %fusion.23), kind=kCustom, calls=%fused_computation.clone | custom fusion | bytes 4202496 | tf_op jit(solution)/shard_map/jit(_take)/gather | solution.py:125
  99.1 2.1 convert_multiply_fusion.4
  101.3 9.3 %gather_fusion.2 = f32[2048,256]{1,0:T(8,128)} fusion(f32[2048,256]{1,0:T(8,128)S(1)} %convert_multiply_fusion.4, s32[2048]{0:T(1024)} %fusion.24), kind=kCustom, calls=%fused_computation.1.clone | custom fusion | bytes 4202496 | tf_op jit(solution)/shard_map/jit(_take)/gather | solution.py:125
  110.5 2.1 convert_multiply_fusion.3
  112.7 9.3 %gather_fusion.3 = f32[2048,256]{1,0:T(8,128)} fusion(f32[2048,256]{1,0:T(8,128)S(1)} %convert_multiply_fusion.3, s32[2048]{0:T(1024)} %fusion.25), kind=kCustom, calls=%fused_computation.2.clone | custom fusion | bytes 4202496 | tf_op jit(solution)/shard_map/jit(_take)/gather | solution.py:125
  122.0 1.8 convert_multiply_fusion.2
  123.8 0.8 gather_fusion
  124.6 1.4 convert_subtract_fusion
  126.0 5.7 fusion.9
  131.7 5.4 copy.48
  137.1 7.7 %tile.11 = bf16[96,64,4,256]{0,1,3,2:T(8,128)(2,1)} broadcast(bf16[96,64,256]{0,1,2:T(8,128)(2,1)} %copy.48), dimensions={0,1,3} | broadcast | bytes 15728640 | tf_op jit(solution)/shard_map/tile | solution.py:15
  144.9 7.3 %all-to-all-start = ((bf16[96,64,1024]{0,1,2:T(8,128)(2,1)}), bf16[96,64,1024]{0,1,2:T(8,128)(2,1)}, u32[]{:S(2)}, u32[]{:S(2)}) async-start(bf16[96,64,1024]{0,1,2:T(8,128)(2,1)} %bitcast.47), calls=%async_computation | async-start | bytes 33554432 | tf_op jit(solution)/shard_map/all_to_all | solution.py:15
  152.6 0.7 convert_convert_fusion
  153.4 182.2 %all-to-all-done = bf16[96,64,1024]{0,1,2:T(8,128)(2,1)} async-done(((bf16[96,64,1024]{0,1,2:T(8,128)(2,1)}), bf16[96,64,1024]{0,1,2:T(8,128)(2,1)}, u32[]{:S(2)}, u32[]{:S(2)}) %all-to-all-start) | async-done | bytes 12582944 | tf_op jit(solution)/shard_map/all_to_all | solution.py:15
  335.6 25.0 %copy.49 = bf16[96,64,1024]{2,1,0:T(8,128)(2,1)} copy(bf16[96,64,1024]{0,1,2:T(8,128)(2,1)} %all-to-all-done) | data formatting | bytes 25165824 | tf_op jit(solution)/shard_map/all_to_all | solution.py:15
  360.6 8.5 %fusion.20 = f32[96,64,256]{2,1,0:T(8,128)S(1)} fusion(bf16[96,64,1024]{2,1,0:T(8,128)(2,1)} %copy.49, s32[256]{0:T(256)S(1)} %copy-done.11, s32[256]{0:T(256)S(1)} %copy-done.9, s32[1024]{0:T(1024)S(1)} %copy-done.13, s32[1024]{0:T(1024)S(1)} %copy-done.12), kind=kOutput, calls=%fused_computation.35 | convolution fusion | flops 3223584768 | bytes 18884608 | tf_op jit(solution)/shard_map/blo,oh->blh/dot_general | solution.py:152
  369.1 28.5 %bitcast_reduce_fusion = f32[96,8,256]{2,1,0:T(8,128)S(1)} fusion(f32[96,64,256]{2,1,0:T(8,128)S(1)} %fusion.20, f32[96,256]{1,0:T(8,128)S(1)} %copy-done.2, f32[96,64]{1,0:T(8,128)S(1)} %copy.51, pred[96,64]{1,0:T(8,128)(4,1)S(1)} %copy.45, bf16[96,64,1024]{2,1,0:T(8,128)(2,1)S(1)} %copy-done, s32[96,1024]{1,0:T(8,128)S(1)} %copy-done.6, ...), kind=kOutput, calls=%fused_computation.15 | convolution fusion | flops 3327983616 | bytes 20805632 | tf_op jit(solution)/shard_map/blo,boh->blh/dot_general | solution.py:149
  397.9 1.7 scatter_custom_fusion
  399.7 60.4 %all_to_all.21 = f32[64,32,256]{2,1,0:T(8,128)} all-to-all(f32[64,32,256]{2,1,0:T(8,128)S(1)} %bitcast.49), channel_id=1, replica_groups=mesh['leaf_0'=8,'leaf_1'=4,'leaf_2'=2,'hand'=4] {'leaf_0','leaf_1','leaf..., dimensions={0} | all-to-all | bytes 4194304 | tf_op jit(solution)/shard_map/all_to_all | solution.py:45
  460.1 1.7 reduce_sum.65
  461.8 1.6 broadcast_in_dim.59
  463.4 7.0 %all-to-all-start.2 = ((f32[64,32,256]{2,1,0:T(8,128)}), f32[64,32,256]{2,1,0:T(8,128)S(1)}, u32[]{:S(2)}, u32[]{:S(2)}) async-start(f32[64,32,256]{2,1,0:T(8,128)} %broadcast_in_dim.59), calls=%async_computation.2 | async-start | bytes 4194304 | tf_op jit(solution)/shard_map/all_to_all | solution.py:51
  470.4 49.7 %all-to-all-done.2 = f32[64,32,256]{2,1,0:T(8,128)S(1)} async-done(((f32[64,32,256]{2,1,0:T(8,128)}), f32[64,32,256]{2,1,0:T(8,128)S(1)}, u32[]{:S(2)}, u32[]{:S(2)}) %all-to-all-start.2) | async-done | bytes 2097184 | tf_op jit(solution)/shard_map/all_to_all | solution.py:51
  520.1 1.3 copy-done.1
  521.5 12.5 %scatter_custom_fusion.1 = f32[2048,256]{1,0:T(8,128)S(1)} fusion(s32[2048]{0:T(1024)} %bitcast.62, f32[2048,256]{1,0:T(8,128)} %bitcast.51, f32[]{:T(128)} %constant.20.clone.1), kind=kCustom, calls=%fused_computation.30 | custom fusion | flops 524288 | bytes 2097664 | tf_op jit(solution)/shard_map/scatter-add | solution.py:169
  534.0 13.0 %scatter_custom_fusion.2 = f32[2048,256]{1,0:T(8,128)} fusion(s32[2048]{0:T(1024)S(1)} %bitcast.59, f32[2048,256]{1,0:T(8,128)S(1)} %scatter_custom_fusion.1, f32[]{:T(128)} %constant.20.clone.1), kind=kCustom, calls=%fused_computation.28 | custom fusion | flops 524288 | bytes 2097156 | tf_op jit(solution)/shard_map/scatter-add | solution.py:169
  546.9 13.3 %scatter_custom_fusion.3 = f32[2048,256]{1,0:T(8,128)} fusion(s32[2048]{0:T(1024)S(1)} %bitcast.56, f32[2048,256]{1,0:T(8,128)} %scatter_custom_fusion.2, f32[]{:T(128)} %constant.20.clone.1), kind=kCustom, calls=%fused_computation.26 | custom fusion | flops 524288 | bytes 2097664 | tf_op jit(solution)/shard_map/scatter-add | solution.py:169
  560.3 0.8 dynamic-slice_reduce_fusion
  561.1 0.7 broadcast_in_dim.96
  561.7 7.0 %all-to-all-start.3 = ((f32[64,1,256]{2,1,0:T(1,128)}), f32[64,1,256]{2,1,0:T(1,128)S(1)}, u32[]{:S(2)}, u32[]{:S(2)}) async-start(f32[64,1,256]{2,1,0:T(1,128)} %broadcast_in_dim.96), calls=%async_computation.3 | async-start | bytes 131072 | tf_op jit(solution)/shard_map/all_to_all | solution.py:51
  568.7 0.8 dynamic-slice_bitcast_fusion
  569.5 0.7 pad_maximum_fusion
  570.1 8.6 %all-to-all-done.3 = f32[64,1,256]{2,1,0:T(1,128)S(1)} async-done(((f32[64,1,256]{2,1,0:T(1,128)}), f32[64,1,256]{2,1,0:T(1,128)S(1)}, u32[]{:S(2)}, u32[]{:S(2)}) %all-to-all-start.3) | async-done | bytes 65568 | tf_op jit(solution)/shard_map/all_to_all | solution.py:51
  578.8 1.2 fusion.26
  580.1 7.5 %all-reduce = (f32[]{:T(128)}, f32[]{:T(128)}) all-reduce(f32[]{:T(128)} %get-tuple-element.5, f32[]{:T(128)} %get-tuple-element.4), channel_id=1, replica_groups=mesh['leaf_0'=8,'leaf_1'=4,'leaf_2'=2,'hand'=4] {'hand'}, use_global_device_ids=true, to_apply=%region_12.14 | all-reduce | flops 2 | bytes 16 | tf_op jit(solution)/shard_map/psum | solution.py:176
  (59 shorter events, 3.1 us)
Async XLA Ops:
  7.2 55.3 %copy-start.15 = (s32[96,8]{0,1:T(8,128)S(1)}, s32[96,8]{0,1:T(8,128)}, u32[]{:S(2)}) copy-start(s32[96,8]{0,1:T(8,128)} %param.24) | copy-start | bytes 9220
  7.2 55.4 %copy-start.19 = (s32[96]{0:T(128)S(1)}, s32[96]{0:T(128)}, u32[]{:S(2)}) copy-start(s32[96]{0:T(128)} %param.22) | copy-start | bytes 1156
  7.2 56.0 %copy-start.14 = (s32[96,5]{0,1:T(8,128)S(1)}, s32[96,5]{0,1:T(8,128)}, u32[]{:S(2)}) copy-start(s32[96,5]{0,1:T(8,128)} %param.20) | copy-start | bytes 5764
  7.2 57.3 %copy-start.7 = (s32[3,2048]{1,0:T(4,128)S(1)}, s32[3,2048]{1,0:T(4,128)}, u32[]{:S(2)}) copy-start(s32[3,2048]{1,0:T(4,128)} %param.19) | copy-start | bytes 73732
  7.2 53.7 %all-gather.4.cloned.1.call-start = ((), (), s32[]{:S(2)}) async-start(), calls=%async_computation.4 | async-start | bytes 2359296 | tf_op jit(solution)/shard_map/all_gather | solution.py:27
  19.9 65.3 %all-gather.6.cloned.1.call-start = ((), (), s32[]{:S(2)}) async-start(), calls=%async_computation.5 | async-start | bytes 6291456 | tf_op jit(solution)/shard_map/all_gather | solution.py:27
  61.7 2.3 copy-start.8
  62.5 1.5 copy-start.10
  64.5 23.3 %copy-start.3 = (s32[1,2048]{1,0:T(1,128)}, s32[1,2048]{1,0:T(1,128)S(1)}, u32[]{:S(2)}) copy-start(s32[1,2048]{1,0:T(1,128)S(1)} %get-tuple-element.15) | copy-start | bytes 24580
  87.9 1.8 copy-start.16
  144.9 7.4 %copy-start.5 = (s32[96,8,8]{0,2,1:T(8,128)S(1)}, s32[96,8,8]{0,2,1:T(8,128)}, u32[]{:S(2)}) copy-start(s32[96,8,8]{0,2,1:T(8,128)} %param.26) | copy-start | bytes 73732
  144.9 7.5 %copy-start.4 = (s32[96,8,8]{0,2,1:T(8,128)S(1)}, s32[96,8,8]{0,2,1:T(8,128)}, u32[]{:S(2)}) copy-start(s32[96,8,8]{0,2,1:T(8,128)} %param.25) | copy-start | bytes 73732
  144.9 7.6 %copy-start.6 = (s32[96,1024]{1,0:T(8,128)S(1)}, s32[96,1024]{1,0:T(8,128)}, u32[]{:S(2)}) copy-start(s32[96,1024]{1,0:T(8,128)} %param.21) | copy-start | bytes 1179652
  144.9 7.6 %copy-start.18 = (s32[96]{0:T(128)S(1)}, s32[96]{0:T(128)}, u32[]{:S(2)}) copy-start(s32[96]{0:T(128)} %param.23) | copy-start | bytes 1156
  144.9 7.7 %copy-start.9 = (s32[256]{0:T(256)S(1)}, s32[256]{0:T(256)}, u32[]{:S(2)}) copy-start(s32[256]{0:T(256)} %copy-done.8) | copy-start | bytes 3076
  144.9 7.7 %copy-start.11 = (s32[256]{0:T(256)S(1)}, s32[256]{0:T(256)}, u32[]{:S(2)}) copy-start(s32[256]{0:T(256)} %copy-done.10) | copy-start | bytes 3076
  144.9 7.7 %copy-start.12 = (s32[1024]{0:T(1024)S(1)}, s32[1024]{0:T(1024)}, u32[]{:S(2)}) copy-start(s32[1024]{0:T(1024)} %constant.77.clone) | copy-start | bytes 12292
  144.9 7.7 %copy-start.13 = (s32[1024]{0:T(1024)S(1)}, s32[1024]{0:T(1024)}, u32[]{:S(2)}) copy-start(s32[1024]{0:T(1024)} %constant.78.clone) | copy-start | bytes 12292
  144.9 190.7 %all-to-all-start = ((bf16[96,64,1024]{0,1,2:T(8,128)(2,1)}), bf16[96,64,1024]{0,1,2:T(8,128)(2,1)}, u32[]{:S(2)}, u32[]{:S(2)}) async-start(bf16[96,64,1024]{0,1,2:T(8,128)(2,1)} %bitcast.47), calls=%async_computation | async-start | bytes 33554432 | tf_op jit(solution)/shard_map/all_to_all | solution.py:15
  360.6 8.5 %copy-start = (bf16[96,64,1024]{2,1,0:T(8,128)(2,1)S(1)}, bf16[96,64,1024]{2,1,0:T(8,128)(2,1)}, u32[]{:S(2)}) copy-start(bf16[96,64,1024]{2,1,0:T(8,128)(2,1)} %copy.49) | copy-start | bytes 37748740
  360.6 8.5 %copy-start.2 = (f32[96,256]{1,0:T(8,128)S(1)}, f32[96,256]{1,0:T(8,128)}, u32[]{:S(2)}) copy-start(f32[96,256]{1,0:T(8,128)} %get-tuple-element.18) | copy-start | bytes 294916
  463.4 56.7 %all-to-all-start.2 = ((f32[64,32,256]{2,1,0:T(8,128)}), f32[64,32,256]{2,1,0:T(8,128)S(1)}, u32[]{:S(2)}, u32[]{:S(2)}) async-start(f32[64,32,256]{2,1,0:T(8,128)} %broadcast_in_dim.59), calls=%async_computation.2 | async-start | bytes 4194304 | tf_op jit(solution)/shard_map/all_to_all | solution.py:51
  520.1 1.4 copy-start.1
  534.0 44.9 %copy-start.17 = (f32[256]{0:T(256)S(1)}, f32[256]{0:T(256)}, u32[]{:S(2)}) copy-start(f32[256]{0:T(256)} %param.17) | copy-start | bytes 3076
  561.7 17.0 %all-to-all-start.3 = ((f32[64,1,256]{2,1,0:T(1,128)}), f32[64,1,256]{2,1,0:T(1,128)S(1)}, u32[]{:S(2)}, u32[]{:S(2)}) async-start(f32[64,1,256]{2,1,0:T(1,128)} %broadcast_in_dim.96), calls=%async_computation.3 | async-start | bytes 131072 | tf_op jit(solution)/shard_map/all_to_all | solution.py:51
Sparse Core Ops, SparseCore 0:
  20.1 40.8 all-gather.3
  62.7 22.4 all-gather.5
